TPU v7x, 512 devices: a whole 4x8x8 slice. The times are simulated.
512 devices in a mesh: seq: 64 (over x, y, core), dp: 8 (over z).
Axes of the slice: x: 4, y: 8, z: 8, core: 2. Of those that a mesh axis runs over, the one named last changes fastest.
Arguments:
- glu_input: bfloat16 [8, 49152, 1024], P('dp', 'seq'), may hold values from -2500 to 2500
- out_grad: bfloat16 [8, 49152, 1024], P('dp', 'seq'), may hold values from -50 to 50
- lengths: int32 [8], replicated, may hold values from 24576 to 49152, as said below
- depth_weight: float32 [512, 31], replicated, may hold values from -1.5 to 1.5
- bn_gain: float32 [512], replicated, may hold values from 0.5 to 2
- bn_shift: float32 [512], replicated, may hold values from -1 to 1
- proj_weight: bfloat16 [512, 1024], P('seq', 'dp'), may hold values from -0.25 to 0.25
Outputs:
- input_grad: bfloat16 [8, 49152, 1024], P('dp', 'seq')
- proj_grad: float32 [512, 1024], P('seq', 'dp')
- depth_grad: float32 [512, 31], P('seq')
- gain_grad: float32 [512], P('seq')
- shift_grad: float32 [512], P('seq')
Inputs may be any that keep to these rules, and one draw needn't show every extreme that they name: `lengths`: at least one utterance has all 49152 frames valid.
All inputs are finite; a program needn't handle non-finite values.
Results may differ from a plain program's by a relative error of at most 0.0061.
Values may be sent and summed in bfloat16 or wider, within the bound.
No kernel may reach another device: no remote copies, remote signals or barrier semaphores. Data moves between devices by JAX's collectives and lax.ppermute only.
A program may use at most 64 MiB of HBM per device.

v0:
```python
import jax
import jax.numpy as jnp
from jax import lax
from jax.sharding import Mesh
from jax.sharding import PartitionSpec as P

SEQ = ("seq_0", "seq_1", "seq_2")
SEQ_DP = ("seq_0", "seq_1", "seq_2", "dp")


EPSILON = 1e-05


def with_halo(block, sides, width):
    for axis, dim in sides:
        count = lax.axis_size(axis)
        forward = [(i, i + 1) for i in range(count - 1)]
        backward = [(target, source) for source, target in forward]
        low = lax.ppermute(
            lax.slice_in_dim(block, block.shape[dim] - width, None, axis=dim), axis, forward
        )
        high = lax.ppermute(lax.slice_in_dim(block, 0, width, axis=dim), axis, backward)
        block = jnp.concatenate([low, block, high], axis=dim)
    return block


def by_axis(array, axes):
    for axis in axes:
        array = lax.psum(array, axis)
    return array


def copy_for_each(array, axis):
    size = lax.axis_size(axis)
    return lax.all_to_all(
        jnp.broadcast_to(array[None], (size, *array.shape)), axis, 0, 0, tiled=True
    )


def in_order(tiles, dim):
    lengths = list(tiles.shape[1:])
    lengths[dim] *= tiles.shape[0]
    return jnp.moveaxis(tiles, 0, dim).reshape(lengths)


def gather_directly(array, axis, dim):
    tiles = copy_for_each(array, axis)
    return in_order(tiles, dim)


def from_behind(block, axis, distance):
    devices = range(lax.axis_size(axis))
    route = [(i - distance, i) for i in devices if i - distance in devices]
    return lax.ppermute(block, axis, route)


def in_blocks(array, dim, size):
    lengths = array.shape
    tiles = array.reshape(*lengths[:dim], size, lengths[dim] // size, *lengths[dim + 1 :])
    return jnp.moveaxis(tiles, dim, 0)


def sum_at_owner(array, axis, dim):
    size = lax.axis_size(axis)
    tiles = lax.all_to_all(in_blocks(array, dim, size), axis, 0, 0, tiled=True)
    return jnp.sum(tiles, axis=0)


def of_everyone(array, axis):
    return copy_for_each(array, axis).sum(axis=0)


def sent_together(arrays, axis, dim, along):
    both = jnp.concatenate(arrays, axis=along)
    out, at, done = (sum_at_owner(both, axis, dim), 0, [])
    for a in arrays:
        done.append(lax.slice_in_dim(out, at, at + a.shape[along], axis=along))
        at += a.shape[along]
    return tuple(done)


def on_device(glu_input, out_grad, lengths, depth_weight, bn_gain, bn_shift, proj_weight):
    utt_dev, frames_dev, doubled = glu_input.shape
    channels = doubled // 2
    kernel = depth_weight.shape[1]
    half_width = (kernel - 1) // 2
    seq_count = lax.axis_size(SEQ)
    grad_scale = float(utt_dev * lax.axis_size("dp") * frames_dev * seq_count) ** (-0.5)
    positions = lax.axis_index(SEQ) * frames_dev + jnp.arange(frames_dev, dtype=jnp.int32)
    own_lengths = lax.dynamic_slice_in_dim(lengths, lax.axis_index("dp") * utt_dev, utt_dev)
    frame_mask = (positions[None, :] < own_lengths[:, None]).astype(jnp.float32)[:, :, None]
    frame_count = jnp.sum(lengths).astype(jnp.float32)
    values = glu_input[:, :, :channels].astype(jnp.float32)
    gate_sigmoid = jax.nn.sigmoid(glu_input[:, :, channels:].astype(jnp.float32))
    glu_out = (values * gate_sigmoid * frame_mask).astype(jnp.bfloat16)
    padded = with_halo(glu_out, ((SEQ, 1),), half_width).astype(jnp.float32)
    conv_out = jnp.zeros((utt_dev, frames_dev, channels), jnp.float32)
    for offset in range(kernel):
        conv_out = conv_out + depth_weight[:, offset] * padded[:, offset : offset + frames_dev]
    conv_total, squares = (
        by_axis(jnp.sum(frame_mask * conv_out, axis=(0, 1)), SEQ_DP),
        by_axis(jnp.sum(frame_mask * conv_out * conv_out, axis=(0, 1)), SEQ_DP),
    )
    mean_val = conv_total / frame_count
    variance = squares / frame_count - mean_val * mean_val
    inv_std = lax.rsqrt(variance + EPSILON)
    normed = (conv_out - mean_val) * inv_std
    pre_act = bn_gain * normed + bn_shift
    pre_sig = jax.nn.sigmoid(pre_act)
    act_out = (frame_mask * pre_act * pre_sig).astype(jnp.bfloat16)
    proj_rows = gather_directly(proj_weight, "dp", 1)
    act_grad = frame_mask * jnp.einsum(
        "btd,cd->btc",
        out_grad,
        gather_directly(proj_rows, SEQ, 0),
        preferred_element_type=jnp.float32,
    )
    pre_grad = act_grad * pre_sig * (1.0 + pre_act * (1.0 - pre_sig))
    gain_sum, shift_sum = (
        by_axis(jnp.sum(pre_grad * normed, axis=(0, 1)), SEQ_DP),
        by_axis(jnp.sum(pre_grad, axis=(0, 1)), SEQ_DP),
    )
    conv_grad = (
        frame_mask
        * inv_std
        * bn_gain
        * (pre_grad - shift_sum / frame_count - normed * gain_sum / frame_count)
    ).astype(jnp.bfloat16)
    conv_wide = conv_grad.astype(jnp.float32)
    weight_terms = (
        jnp.einsum("btc,btd->cd", act_out, out_grad, preferred_element_type=jnp.float32)
        * grad_scale
    )
    depth_terms = (
        jnp.stack(
            [
                jnp.sum(conv_wide * padded[:, offset : offset + frames_dev], axis=(0, 1))
                for offset in range(kernel)
            ],
            axis=1,
        )
        * grad_scale
    )
    local_pad = jnp.pad(conv_wide, ((0, 0), (2 * half_width, 2 * half_width), (0, 0)))
    widened = jnp.zeros((utt_dev, frames_dev + 2 * half_width, channels), jnp.float32)
    for offset in range(kernel):
        widened = (
            widened
            + depth_weight[:, offset]
            * local_pad[:, 2 * half_width - offset : 4 * half_width - offset + frames_dev]
        )
    own_rows = widened[:, half_width : half_width + frames_dev]
    from_right = from_behind(widened[:, :half_width], SEQ, -1)
    from_left = from_behind(widened[:, half_width + frames_dev :], SEQ, 1)
    own_rows = own_rows.at[:, frames_dev - half_width :].add(from_right)
    glu_grad = own_rows.at[:, :half_width].add(from_left)
    glu_grad = glu_grad * frame_mask
    input_grad = jnp.concatenate(
        [glu_grad * gate_sigmoid, glu_grad * values * gate_sigmoid * (1.0 - gate_sigmoid)], axis=2
    ).astype(jnp.bfloat16)
    proj_part = sum_at_owner(weight_terms, "dp", 1)
    depth_part = of_everyone(depth_terms, "dp")
    proj_grad, depth_grad = sent_together((proj_part, depth_part), SEQ, 0, 1)
    per_device = channels // seq_count
    first_channel = lax.axis_index(SEQ) * per_device
    gain_grad = lax.dynamic_slice_in_dim(gain_sum, first_channel, per_device) * grad_scale
    shift_grad = lax.dynamic_slice_in_dim(shift_sum, first_channel, per_device) * grad_scale
    return (input_grad, proj_grad, depth_grad, gain_grad, shift_grad)


def solution(mesh):
    finer = Mesh(mesh.devices.reshape(4, 8, 2, mesh.shape["dp"]), ("seq_0", "seq_1", "seq_2", "dp"))
    return jax.shard_map(
        on_device,
        mesh=finer,
        in_specs=(P("dp", SEQ, None), P("dp", SEQ, None), P(), P(), P(), P(), P(SEQ, "dp")),
        out_specs=(P("dp", SEQ, None), P(SEQ, "dp"), P(SEQ, None), P(SEQ), P(SEQ)),
        check_vma=False,
    )
```

profile of v0, /device:TPU:1, one launch (start us, length us, event | category | flops | bytes accessed | tf_op | source)
XLA Modules:
  0.0 251.7 jit_solution(9465287463388099233)
XLA Ops:
  0.6 0.0 copy-start
  0.6 0.0 copy-start.8
  0.7 1.4 broadcast_in_dim.8
  2.1 10.9 %all-to-all-start = ((bf16[8,8,128]{2,1,0:T(8,128)(2,1)}), bf16[8,8,128]{2,1,0:T(8,128)(2,1)S(1)}, u32[]{:S(2)}, u32[]{:S(2)}) async-start(bf16[8,8,128]{2,1,0:T(8,128)(2,1)} %broadcast_in_dim.8), calls=%async_computation | async-start | bytes 32768 | tf_op jit(solution)/shard_map/all_to_all | solution.py:35
  12.9 1.2 dynamic_slice.9
  14.2 0.6 fusion.51
  14.8 1.8 fusion.2
  16.7 0.0 copy-start.4
  16.7 0.9 copy-done.4
  17.6 4.0 %collective-permute-start = (bf16[1,15,512]{2,1,0:T(8,128)(2,1)S(1)}, bf16[1,15,512]{2,1,0:T(8,128)(2,1)S(1)}, u32[]{:S(2)}, u32[]{:S(2)}) collective-permute-start(bf16[1,15,512]{2,1,0:T(8,128)(2,1)S(1)} %get-tuple-element.86), channel_id=1, source_target_pairs={{0,8},{8,16},{16,24},{24,32},{32,40},{40,48},{48,56},{56,64},{64,7... | collective-permute-start | bytes 46088 | tf_op jit(solution)/shard_map/ppermute | solution.py:19
  21.6 1.9 collective-permute-start.1
  23.6 0.0 copy-done.8
  23.6 0.6 reduce_sum.352
  24.9 0.0 collective-permute-done
  24.9 1.7 collective-permute-done.1
  26.7 1.4 maximum_convert_fusion
  28.0 0.0 all-to-all-done
  28.0 1.1 broadcast_in_dim.10
  29.2 10.6 %all-to-all-start.1 = ((bf16[64,8,1024]{2,1,0:T(8,128)(2,1)}), bf16[64,8,1024]{2,1,0:T(8,128)(2,1)}, u32[]{:S(2)}, u32[]{:S(2)}) async-start(bf16[64,8,1024]{2,1,0:T(8,128)(2,1)} %broadcast_in_dim.10), calls=%async_computation.1 | async-start | bytes 2097152 | tf_op jit(solution)/shard_map/all_to_all | solution.py:35
  39.8 0.0 copy-start.6
  39.8 0.0 copy-start.7
  39.8 7.4 %fusion.6 = (f32[512]{0:T(512)S(1)}, f32[512]{0:T(512)S(1)}, f32[1,768,512]{2,1,0:T(8,128)}) fusion(f32[768]{0:T(1024)S(1)} %fusion.51, f32[1,798,512]{2,1,0:T(8,128)S(1)} %maximum_convert_fusion, f32[512]{0:T(512)S(1)} %bitcast.157, f32[512]{0:T(512)S(1)} %bitcast.159, f32[512]{0:T(512)S(1)} %bitcast.101, f32[512]{0:T(512)S(1)} %bitcast.103, ...), kind=kLoop, calls=%fused_computation.45 | loop fusion | flops 25558016 | bytes 50402304 | tf_op jit(solution)/shard_map/reduce_sum | solution.py:102
  47.2 9.9 %all-reduce.6 = (f32[512]{0:T(512)S(1)}, f32[512]{0:T(512)S(1)}) all-reduce(f32[512]{0:T(512)S(1)} %get-tuple-element.61, f32[512]{0:T(512)S(1)} %get-tuple-element.60), channel_id=1, replica_groups=mesh['seq_0'=4,'seq_1'=8,'seq_2'=2,'dp'=8] {'seq_0'}, use_global_device_ids=true, to_apply=%region_7.0 | all-reduce | flops 1024 | bytes 8192 | tf_op jit(solution)/shard_map/psum | solution.py:29
  57.1 15.4 %all-reduce.4 = (f32[512]{0:T(512)S(1)}, f32[512]{0:T(512)S(1)}) all-reduce(f32[512]{0:T(512)S(1)} %get-tuple-element.74, f32[512]{0:T(512)S(1)} %get-tuple-element.75), channel_id=1, replica_groups=mesh['seq_0'=4,'seq_1'=8,'seq_2'=2,'dp'=8] {'seq_1'}, use_global_device_ids=true, to_apply=%region_8.0 | all-reduce | flops 1024 | bytes 8192 | tf_op jit(solution)/shard_map/psum | solution.py:29
  72.5 5.0 %all-reduce.8 = (f32[512]{0:T(512)S(1)}, f32[512]{0:T(512)S(1)}) all-reduce(f32[512]{0:T(512)S(1)} %get-tuple-element.70, f32[512]{0:T(512)S(1)} %get-tuple-element.71), channel_id=1, replica_groups=mesh['seq_0'=4,'seq_1'=8,'seq_2'=2,'dp'=8] {'seq_2'}, use_global_device_ids=true, to_apply=%region_9.0 | all-reduce | flops 1024 | bytes 8192 | tf_op jit(solution)/shard_map/psum | solution.py:29
  77.5 13.6 %all-reduce.2 = (f32[512]{0:T(512)S(1)}, f32[512]{0:T(512)S(1)}) all-reduce(f32[512]{0:T(512)S(1)} %get-tuple-element.78, f32[512]{0:T(512)S(1)} %get-tuple-element.79), channel_id=1, replica_groups=mesh['seq_0'=4,'seq_1'=8,'seq_2'=2,'dp'=8] {'dp'}, use_global_device_ids=true, to_apply=%region_10.0 | all-reduce | flops 1024 | bytes 8192 | tf_op jit(solution)/shard_map/psum | solution.py:29
  91.1 0.0 all-to-all-done.1
  91.2 4.5 %fusion.53 = (f32[512]{0:T(512)S(1)}, f32[512]{0:T(512)S(1)}, f32[1,768,512]{2,1,0:T(8,128)}) fusion(f32[512]{0:T(512)S(1)} %get-tuple-element.119, f32[1,768,512]{2,1,0:T(8,128)} %get-tuple-element.81, f32[512]{0:T(512)S(1)} %get-tuple-element.120, f32[512]{0:T(512)S(1)} %copy-done.7, f32[512]{0:T(512)S(1)} %copy-done.6, ...), kind=kOutput, calls=%fused_computation.113 | convolution fusion | flops 811596800 | bytes 5782528 | tf_op jit(solution)/shard_map/btd,cd->btc/dot_general | solution.py:112
  95.7 8.6 %all-reduce.5 = (f32[512]{0:T(512)S(1)}, f32[512]{0:T(512)S(1)}) all-reduce(f32[512]{0:T(512)S(1)} %get-tuple-element.63, f32[512]{0:T(512)S(1)} %get-tuple-element.62), channel_id=1, replica_groups=mesh['seq_0'=4,'seq_1'=8,'seq_2'=2,'dp'=8] {'seq_0'}, use_global_device_ids=true, to_apply=%region_17.0 | all-reduce | flops 1024 | bytes 8192 | tf_op jit(solution)/shard_map/psum | solution.py:29
  104.3 11.2 %all-reduce.3 = (f32[512]{0:T(512)S(1)}, f32[512]{0:T(512)S(1)}) all-reduce(f32[512]{0:T(512)S(1)} %get-tuple-element.72, f32[512]{0:T(512)S(1)} %get-tuple-element.73), channel_id=1, replica_groups=mesh['seq_0'=4,'seq_1'=8,'seq_2'=2,'dp'=8] {'seq_1'}, use_global_device_ids=true, to_apply=%region_18.0 | all-reduce | flops 1024 | bytes 8192 | tf_op jit(solution)/shard_map/psum | solution.py:29
  115.5 11.7 %all-reduce.7 = (f32[512]{0:T(512)S(1)}, f32[512]{0:T(512)S(1)}) all-reduce(f32[512]{0:T(512)S(1)} %get-tuple-element.68, f32[512]{0:T(512)S(1)} %get-tuple-element.69), channel_id=1, replica_groups=mesh['seq_0'=4,'seq_1'=8,'seq_2'=2,'dp'=8] {'seq_2'}, use_global_device_ids=true, to_apply=%region_19.0 | all-reduce | flops 1024 | bytes 8192 | tf_op jit(solution)/shard_map/psum | solution.py:29
  127.2 11.6 %all-reduce.1 = (f32[512]{0:T(512)S(1)}, f32[512]{0:T(512)S(1)}) all-reduce(f32[512]{0:T(512)S(1)} %get-tuple-element.76, f32[512]{0:T(512)S(1)} %get-tuple-element.77), channel_id=1, replica_groups=mesh['seq_0'=4,'seq_1'=8,'seq_2'=2,'dp'=8] {'dp'}, use_global_device_ids=true, to_apply=%region_20.0 | all-reduce | flops 1024 | bytes 8192 | tf_op jit(solution)/shard_map/psum | solution.py:29
  138.9 4.8 %fusion.36 = (f32[512]{0:T(512)S(1)}, f32[512]{0:T(512)S(1)}, f32[512]{0:T(512)S(1)}, f32[512]{0:T(512)S(1)}, f32[512]{0:T(512)S(1)}, /*index=5*/f32[512]{0:T(51...) fusion(f32[1,798,512]{2,1,0:T(8,128)S(1)} %maximum_convert_fusi, ...), kind=kLoop, calls=%fused_computation.75 | loop fusion | flops 14542336 | bytes 24419332 | tf_op jit(solution)/shard_map/reduce_sum | solution.py:137
  143.7 3.6 %fusion.37 = (f32[512]{0:T(512)S(1)}, f32[512]{0:T(512)S(1)}, f32[512]{0:T(512)S(1)}, f32[512]{0:T(512)S(1)}, f32[512]{0:T(512)S(1)}, /*index=5*/f32[512]{0:T(51...) fusion(bf16[1,768,512]{2,1,0:T(8,128)(2,1)S(1)} %get-tuple-elem, ...), kind=kLoop, calls=%fused_computation.76 | loop fusion | flops 14539776 | bytes 29134848 | tf_op jit(solution)/shard_map/reduce_sum | solution.py:137
  147.4 0.0 copy-start.3
  147.4 0.1 stack.127
  147.5 0.9 broadcast_in_dim.11
  148.4 4.5 %all-to-all-start.3 = ((f32[8,512,31]{1,2,0:T(8,128)}), f32[8,512,31]{1,2,0:T(8,128)}, u32[]{:S(2)}, u32[]{:S(2)}) async-start(f32[8,512,31]{1,2,0:T(8,128)} %broadcast_in_dim.11), calls=%async_computation.3 | async-start | bytes 1048576 | tf_op jit(solution)/shard_map/all_to_all | solution.py:35
  152.9 1.1 multiply_bitcast_fusion
  154.0 1.5 copy.20
  155.5 9.2 %all-to-all-done.3 = f32[8,512,31]{1,2,0:T(8,128)} async-done(((f32[8,512,31]{1,2,0:T(8,128)}), f32[8,512,31]{1,2,0:T(8,128)}, u32[]{:S(2)}, u32[]{:S(2)}) %all-to-all-start.3) | async-done | bytes 507936 | tf_op jit(solution)/shard_map/all_to_all | solution.py:35
  164.7 4.7 %all-to-all-start.2 = ((f32[8,512,128]{2,1,0:T(8,128)}), f32[8,512,128]{2,1,0:T(8,128)}, u32[]{:S(2)}, u32[]{:S(2)}) async-start(f32[8,512,128]{2,1,0:T(8,128)} %bitcast.97), calls=%async_computation.2 | async-start | bytes 4194304 | tf_op jit(solution)/shard_map/all_to_all | solution.py:65
  169.4 0.2 convert_element_type.59
  169.6 6.1 %multiply_add_fusion = f32[1,798,512]{2,1,0:T(8,128)S(1)} fusion(f32[1,768,512]{2,1,0:T(8,128)S(1)} %convert_element_type.59, f32[512]{0:T(512)S(1)} %bitcast.158, f32[512]{0:T(512)S(1)} %bitcast.160, f32[512]{0:T(512)S(1)} %bitcast.102, f32[512]{0:T(512)S(1)} %bitcast.104, f32[512]{0:T(512)S(1)} %bitcast.106, f32[512]{0:T(512)S(1)} %bitcast.108, ...), kind=kLoop, calls=%fused_computation.37 | loop fusion | flops 24923136 | bytes 3270656 | tf_op jit(solution)/shard_map/add | solution.py:148
  175.8 8.6 %collective-permute-start.2 = (f32[1,15,512]{2,1,0:T(8,128)S(1)}, f32[1,15,512]{2,1,0:T(8,128)S(1)}, u32[]{:S(2)}, u32[]{:S(2)}) collective-permute-start(f32[1,15,512]{2,1,0:T(8,128)S(1)} %get-tuple-element.85), channel_id=1, source_target_pairs={{8,0},{16,8},{24,16},{32,24},{40,32},{48,40},{56,48},{64,56},{72,6... | collective-permute-start | bytes 92168 | tf_op jit(solution)/shard_map/ppermute | solution.py:54
  184.4 0.6 dynamic-slice_multiply_fusion
  185.0 0.2 slice.554
  185.2 3.0 %collective-permute-start.3 = (f32[1,15,512]{2,1,0:T(8,128)S(1)}, f32[1,15,512]{2,1,0:T(8,128)S(1)}, u32[]{:S(2)}, u32[]{:S(2)}) collective-permute-start(f32[1,15,512]{2,1,0:T(8,128)S(1)} %get-tuple-element.84), channel_id=1, source_target_pairs={{0,8},{8,16},{16,24},{24,32},{32,40},{40,48},{48,56},{56,64},{64,7... | collective-permute-start | bytes 92168 | tf_op jit(solution)/shard_map/ppermute | solution.py:54
  188.2 0.0 collective-permute-done.2
  188.2 0.2 scatter-add.6
  188.5 1.1 reduce_sum.388
  189.6 0.8 copy.17
  190.4 24.9 %all-to-all-done.2 = f32[8,512,128]{2,1,0:T(8,128)} async-done(((f32[8,512,128]{2,1,0:T(8,128)}), f32[8,512,128]{2,1,0:T(8,128)}, u32[]{:S(2)}, u32[]{:S(2)}) %all-to-all-start.2) | async-done | bytes 2097184 | tf_op jit(solution)/shard_map/all_to_all | solution.py:65
  215.3 1.7 reduce_sum.356
  217.1 1.8 maximum_bitcast_fusion
  218.9 13.4 %all-to-all-start.4 = ((f32[64,8,159]{2,1,0:T(8,128)}), f32[64,8,159]{2,1,0:T(8,128)}, u32[]{:S(2)}, u32[]{:S(2)}) async-start(f32[64,8,159]{2,1,0:T(8,128)} %maximum_bitcast_fusion), calls=%async_computation.4 | async-start | bytes 1048576 | tf_op jit(solution)/shard_map/all_to_all | solution.py:65
  232.2 0.0 collective-permute-done.3
  232.3 0.3 scatter-add.9
  232.6 2.1 multiply_convert_fusion.1
  234.7 1.4 pad_maximum_fusion
  236.1 13.4 %all-to-all-done.4 = f32[64,8,159]{2,1,0:T(8,128)} async-done(((f32[64,8,159]{2,1,0:T(8,128)}), f32[64,8,159]{2,1,0:T(8,128)}, u32[]{:S(2)}, u32[]{:S(2)}) %all-to-all-start.4) | async-done | bytes 325664 | tf_op jit(solution)/shard_map/all_to_all | solution.py:65
  249.4 1.1 reduce_sum.389
  250.6 0.6 slice.560
  251.2 0.6 slice.559
  (19 shorter events, 0.1 us)
Async XLA Ops:
  0.6 90.5 %copy-start = (bf16[1,768,1024]{2,1,0:T(8,128)(2,1)S(1)}, bf16[1,768,1024]{2,1,0:T(8,128)(2,1)}, u32[]{:S(2)}) copy-start(bf16[1,768,1024]{2,1,0:T(8,128)(2,1)} %param.12) | copy-start | bytes 4718596
  0.6 23.0 %copy-start.8 = (s32[8]{0:T(128)S(1)}, s32[8]{0:T(128)}, u32[]{:S(2)}) copy-start(s32[8]{0:T(128)} %param.13) | copy-start | bytes 100
  0.7 22.9 %copy-start.5 = (f32[512,31]{0,1:T(8,128)S(1)}, f32[512,31]{0,1:T(8,128)}, u32[]{:S(2)}) copy-start(f32[512,31]{0,1:T(8,128)} %param.14) | copy-start | bytes 190468
  2.1 25.9 %all-to-all-start = ((bf16[8,8,128]{2,1,0:T(8,128)(2,1)}), bf16[8,8,128]{2,1,0:T(8,128)(2,1)S(1)}, u32[]{:S(2)}, u32[]{:S(2)}) async-start(bf16[8,8,128]{2,1,0:T(8,128)(2,1)} %broadcast_in_dim.8), calls=%async_computation | async-start | bytes 32768 | tf_op jit(solution)/shard_map/all_to_all | solution.py:35
  16.7 0.9 copy-start.4
  17.6 7.3 %collective-permute-start = (bf16[1,15,512]{2,1,0:T(8,128)(2,1)S(1)}, bf16[1,15,512]{2,1,0:T(8,128)(2,1)S(1)}, u32[]{:S(2)}, u32[]{:S(2)}) collective-permute-start(bf16[1,15,512]{2,1,0:T(8,128)(2,1)S(1)} %get-tuple-element.86), channel_id=1, source_target_pairs={{0,8},{8,16},{16,24},{24,32},{32,40},{40,48},{48,56},{56,64},{64,7... | collective-permute-start | bytes 46088 | tf_op jit(solution)/shard_map/ppermute | solution.py:19
  21.6 5.1 %collective-permute-start.1 = (bf16[1,15,512]{2,1,0:T(8,128)(2,1)S(1)}, bf16[1,15,512]{2,1,0:T(8,128)(2,1)S(1)}, u32[]{:S(2)}, u32[]{:S(2)}) collective-permute-start(bf16[1,15,512]{2,1,0:T(8,128)(2,1)S(1)} %get-tuple-element.87), channel_id=1, source_target_pairs={{8,0},{16,8},{24,16},{32,24},{40,32},{48,40},{56,48},{64,56},{72,6... | collective-permute-start | bytes 46088 | tf_op jit(solution)/shard_map/ppermute | solution.py:22
  29.2 62.0 %all-to-all-start.1 = ((bf16[64,8,1024]{2,1,0:T(8,128)(2,1)}), bf16[64,8,1024]{2,1,0:T(8,128)(2,1)}, u32[]{:S(2)}, u32[]{:S(2)}) async-start(bf16[64,8,1024]{2,1,0:T(8,128)(2,1)} %broadcast_in_dim.10), calls=%async_computation.1 | async-start | bytes 2097152 | tf_op jit(solution)/shard_map/all_to_all | solution.py:35
  39.8 51.4 %copy-start.6 = (f32[512]{0:T(512)S(1)}, f32[512]{0:T(512)}, u32[]{:S(2)}) copy-start(f32[512]{0:T(512)} %param.15) | copy-start | bytes 6148
  39.8 51.4 %copy-start.7 = (f32[512]{0:T(512)S(1)}, f32[512]{0:T(512)}, u32[]{:S(2)}) copy-start(f32[512]{0:T(512)} %param.16) | copy-start | bytes 6148
  143.7 3.6 %copy-start.1 = (bf16[1,768,512]{2,1,0:T(8,128)(2,1)}, bf16[1,768,512]{2,1,0:T(8,128)(2,1)S(1)}, u32[]{:S(2)}) copy-start(bf16[1,768,512]{2,1,0:T(8,128)(2,1)S(1)} %get-tuple-element.80) | copy-start | bytes 2359300
  147.4 5.5 %copy-start.3 = (f32[1,768,512]{2,1,0:T(8,128)S(1)}, f32[1,768,512]{2,1,0:T(8,128)}, u32[]{:S(2)}) copy-start(f32[1,768,512]{2,1,0:T(8,128)} %get-tuple-element.81) | copy-start | bytes 4718596
  148.4 16.3 %all-to-all-start.3 = ((f32[8,512,31]{1,2,0:T(8,128)}), f32[8,512,31]{1,2,0:T(8,128)}, u32[]{:S(2)}, u32[]{:S(2)}) async-start(f32[8,512,31]{1,2,0:T(8,128)} %broadcast_in_dim.11), calls=%async_computation.3 | async-start | bytes 1048576 | tf_op jit(solution)/shard_map/all_to_all | solution.py:35
  164.7 4.7 %copy-start.2 = (bf16[1,768,512]{2,1,0:T(8,128)(2,1)S(1)}, bf16[1,768,512]{2,1,0:T(8,128)(2,1)}, u32[]{:S(2)}) copy-start(bf16[1,768,512]{2,1,0:T(8,128)(2,1)} %copy-done.1) | copy-start | bytes 2359300
  164.7 50.7 %all-to-all-start.2 = ((f32[8,512,128]{2,1,0:T(8,128)}), f32[8,512,128]{2,1,0:T(8,128)}, u32[]{:S(2)}, u32[]{:S(2)}) async-start(f32[8,512,128]{2,1,0:T(8,128)} %bitcast.97), calls=%async_computation.2 | async-start | bytes 4194304 | tf_op jit(solution)/shard_map/all_to_all | solution.py:65
  175.8 12.4 %collective-permute-start.2 = (f32[1,15,512]{2,1,0:T(8,128)S(1)}, f32[1,15,512]{2,1,0:T(8,128)S(1)}, u32[]{:S(2)}, u32[]{:S(2)}) collective-permute-start(f32[1,15,512]{2,1,0:T(8,128)S(1)} %get-tuple-element.85), channel_id=1, source_target_pairs={{8,0},{16,8},{24,16},{32,24},{40,32},{48,40},{56,48},{64,56},{72,6... | collective-permute-start | bytes 92168 | tf_op jit(solution)/shard_map/ppermute | solution.py:54
  185.2 47.0 %collective-permute-start.3 = (f32[1,15,512]{2,1,0:T(8,128)S(1)}, f32[1,15,512]{2,1,0:T(8,128)S(1)}, u32[]{:S(2)}, u32[]{:S(2)}) collective-permute-start(f32[1,15,512]{2,1,0:T(8,128)S(1)} %get-tuple-element.84), channel_id=1, source_target_pairs={{0,8},{8,16},{16,24},{24,32},{32,40},{40,48},{48,56},{56,64},{64,7... | collective-permute-start | bytes 92168 | tf_op jit(solution)/shard_map/ppermute | solution.py:54
  218.9 30.6 %all-to-all-start.4 = ((f32[64,8,159]{2,1,0:T(8,128)}), f32[64,8,159]{2,1,0:T(8,128)}, u32[]{:S(2)}, u32[]{:S(2)}) async-start(f32[64,8,159]{2,1,0:T(8,128)} %maximum_bitcast_fusion), calls=%async_computation.4 | async-start | bytes 1048576 | tf_op jit(solution)/shard_map/all_to_all | solution.py:65
where the time goes:
time: 253 us; the launch traced here: 252 us
  blocking collectives  87.1 us (34%)
  starting transfers between devices  61.6 us (24%)
  waiting for transfers between devices  49.2 us (19%)
  other arithmetic  36.5 us (14%)
  local copies, waits for them, and re-layouts  10.1 us (4%)
  matrix products  5.66 us (2%)
    psum x8, blocking collectives, by_axis(): array = lax.psum(array, axis)  87.1 us
    all_to_all x2, waiting for transfers between devices, sum_at_owner(): tiles = lax.all_to_all(in_blocks(array, dim, size), axis, 0, 0, tiled=True)  38.3 us
    all_to_all x3, starting transfers between devices, copy_for_each(): lax.all_to_all(jnp.broadcast_to(array[None], (size, *array.shape)), axis,...  25.9 us
    all_to_all x2, starting transfers between devices, sum_at_owner(): tiles = lax.all_to_all(in_blocks(array, dim, size), axis, 0, 0, tiled=True)  18.1 us
    ppermute x2, starting transfers between devices, from_behind(): return lax.ppermute(block, axis, route)  11.6 us
    all_to_all x3, waiting for transfers between devices, copy_for_each(): lax.all_to_all(jnp.broadcast_to(array[None], (size, *array.shape)), axis,...  9.18 us
    reduce_sum x2, other arithmetic, on_device(): jnp.sum(conv_wide * padded[:, offset:offset + frames_dev], axis=(0, 1))  8.46 us
    reduce_sum x1, other arithmetic, on_device(): jnp.sum(frame_mask * conv_out * conv_out, axis=(0, 1))  7.4 us
  transfers between devices with their start and end apart: 9, of which 4 were waited for; matrix products, arithmetic and copies ran while one was open for 13% of the time, Pallas kernels for 0%

commit v1 on v0

v1 whole, which is shorter than its diff:
```python
import functools
import math

import jax
import jax.numpy as jnp
from jax import lax
from jax.experimental import pallas as pl
from jax.experimental.pallas import tpu as pltpu
from jax.sharding import Mesh
from jax.sharding import PartitionSpec as P

XY = ("seq_0", "seq_1")
SEQ = ("seq_0", "seq_1", "seq_2")
CORE_DP = ("seq_2", "dp")

EPSILON = 1e-05
TAPS = 31
HALF = 15
EDGE = 16
WIDE = 32
LANES = 128

F32 = jnp.float32
BF16 = jnp.bfloat16


def sigmoid(x):
    return 0.5 + 0.5 * jnp.tanh(0.5 * x)


def rows_per_step(rows):
    return max(r for r in range(8, 97, 8) if rows % r == 0)


def rows_iota(rows):
    return lax.broadcasted_iota(jnp.int32, (rows, LANES), 0)


def fold(x):
    return jnp.sum(x.reshape(x.shape[0] // 8, 8, LANES), axis=0)


def shifted_taps(read, rows, combine):
    for residue in range(8):
        block = read(residue, rows + 24)
        for step in range(4):
            k = 8 * step + residue - 1
            if 0 <= k < TAPS:
                combine(k, block[8 * step : 8 * step + rows])


def glu_kernel(meta, val, gate, low_val, low_gate, high_val, high_gate, taps, glu, conv, stats):
    frames = val.shape[0]
    first, length = meta[0], meta[1]

    def put(at, rows, v, g):
        pos = first - WIDE + at + rows_iota(rows)
        ok = (pos >= 0) & (pos < length)
        out = jnp.where(ok, v.astype(F32) * sigmoid(g.astype(F32)), 0.0)
        glu[pl.ds(at, rows), :] = out.astype(BF16).astype(F32)

    put(0, WIDE, low_val[0:WIDE, :], low_gate[0:WIDE, :])
    put(WIDE + frames, WIDE, high_val[0:WIDE, :], high_gate[0:WIDE, :])
    part = rows_per_step(frames)
    part = part if part % 16 == 0 else frames

    def put_own(i, _):
        at = pl.multiple_of(i * part, 16)
        put(WIDE + at, part, val[pl.ds(at, part), :], gate[pl.ds(at, part), :])
        return 0

    lax.fori_loop(0, frames // part, put_own, 0)

    total = frames + 2 * EDGE
    rows = rows_per_step(total)

    def step(i, carry):
        at = pl.multiple_of(i * rows, 8)
        acc = [jnp.zeros((rows, LANES), F32)]

        def add(k, window):
            acc[0] = acc[0] + taps[k : k + 1, :] * window

        shifted_taps(lambda s, n: glu[pl.ds(at + s, n), :], rows, add)
        conv[pl.ds(at, rows), :] = acc[0]
        idx = at + rows_iota(rows)
        own = (idx >= EDGE) & (idx < EDGE + frames) & (first - EDGE + idx < length)
        kept = jnp.where(own, acc[0], 0.0)
        return carry[0] + fold(kept), carry[1] + fold(kept * kept)

    zero = jnp.zeros((8, LANES), F32)
    s, q = lax.fori_loop(0, total // rows, step, (zero, zero))
    stats[0:1, :] = jnp.sum(s, axis=0, keepdims=True)
    stats[1:2, :] = jnp.sum(q, axis=0, keepdims=True)


def correlate(first, length, frames, source, glu, acc):
    rows = rows_per_step(frames)
    acc[...] = jnp.zeros_like(acc)

    def step(i, _):
        at = pl.multiple_of(i * rows, 8)
        ok = first + at + rows_iota(rows) < length
        mine = jnp.where(ok, source[pl.ds(EDGE + at, rows), :], 0.0)

        def add(k, window):
            acc[8 * k : 8 * k + 8, :] += fold(mine * window)

        shifted_taps(lambda s, n: glu[pl.ds(EDGE + at + s, n), :], rows, add)
        return 0

    lax.fori_loop(0, frames // rows, step, 0)


def spread(acc):
    return jnp.sum(acc[...].reshape(TAPS + 1, 8, LANES), axis=1)


def early_kernel(meta, glu, conv, out, acc):
    frames = conv.shape[0] - 2 * EDGE
    first, length = meta[0], meta[1]
    shape = (TAPS + 1, frames + 2 * WIDE)
    frame = (
        lax.broadcasted_iota(jnp.int32, shape, 1)
        - lax.broadcasted_iota(jnp.int32, shape, 0)
        - (EDGE + 1)
    )
    pick = (frame >= 0) & (frame < frames) & (first + frame < length)
    out[0] = jnp.dot(
        jnp.where(pick, 1.0, 0.0).astype(BF16), glu[...].astype(BF16), preferred_element_type=F32
    )
    correlate(first, length, frames, conv, glu, acc)
    out[1] = spread(acc)


def depth_kernel(meta, glu, pre_grad, out, acc):
    frames = pre_grad.shape[0] - 2 * EDGE
    correlate(meta[0], meta[1], frames, pre_grad, glu, acc)
    out[...] = spread(acc)


def act_grad_kernel(grad, low, high, weight, out):
    frames = grad.shape[0]
    side = jnp.concatenate([weight[z] for z in range(weight.shape[0])], axis=1)
    dims = (((1,), (1,)), ((), ()))
    edges = jnp.concatenate([low[WIDE : WIDE + EDGE, :], high[WIDE : WIDE + EDGE, :]], axis=0)
    both = lax.dot_general(edges, side, dims, preferred_element_type=F32)
    out[0:EDGE, :] = both[0:EDGE]
    out[EDGE + frames :, :] = both[EDGE:]
    out[EDGE : EDGE + frames, :] = lax.dot_general(grad[...], side, dims, preferred_element_type=F32)


def moments(stats, count, tmp):
    j = pl.program_id(0)
    tmp[...] = jnp.sum(stats[...], axis=0)
    mean = tmp[pl.ds(j, 1), :] / count
    var = tmp[pl.ds(j + 4, 1), :] / count - mean * mean
    return mean, lax.rsqrt(var + EPSILON)


def pre_kernel(meta, stats, count, gain, shift, conv, act_grad, act, pre_grad, sums, tmp):
    frames = conv.shape[0] - 2 * EDGE
    total = frames + 2 * EDGE
    first, length = meta[0], meta[1]
    mean, inv = moments(stats, count[0:1, :], tmp)
    g, b = gain[...], shift[...]

    def piece(at, rows, keep_act):
        normed = (conv[pl.ds(at, rows), :] - mean) * inv
        pre = g * normed + b
        sig = sigmoid(pre)
        pos = first - EDGE + at + rows_iota(rows)
        ok = (pos >= 0) & (pos < length)
        gone = jnp.where(ok, act_grad[pl.ds(at, rows), :] * sig * (1.0 + pre * (1.0 - sig)), 0.0)
        pre_grad[pl.ds(at, rows), :] = gone
        if keep_act:
            act[pl.ds(at - EDGE, rows), :] = jnp.where(ok, pre * sig, 0.0).astype(BF16)
        return gone, gone * normed

    piece(0, EDGE, False)
    piece(EDGE + frames, EDGE, False)
    rows = rows_per_step(frames)
    rows = rows if rows % 16 == 0 else frames

    def step(i, carry):
        one, two = piece(pl.multiple_of(EDGE + i * rows, 16), rows, True)
        return carry[0] + fold(two), carry[1] + fold(one)

    zero = jnp.zeros((8, LANES), F32)
    gs, ss = lax.fori_loop(0, frames // rows, step, (zero, zero))
    sums[0:1, :] = jnp.sum(gs, axis=0, keepdims=True)
    sums[1:2, :] = jnp.sum(ss, axis=0, keepdims=True)


def last_kernel(
    meta, stats, count, gain, sums, taps, conv, pre_grad, val, gate, out_val, out_gate, cg, tmp
):
    frames = val.shape[0]
    total = frames + 2 * EDGE
    first, length = meta[0], meta[1]
    n = count[0:1, :]
    mean, inv = moments(stats, n, tmp)
    scale = inv * gain[...]
    gm, sm = sums[0:1, :] / n, sums[1:2, :] / n
    rows = rows_per_step(total)

    def grad(i, _):
        at = pl.multiple_of(i * rows, 8)
        normed = (conv[pl.ds(at, rows), :] - mean) * inv
        pos = first - EDGE + at + rows_iota(rows)
        ok = (pos >= 0) & (pos < length)
        full = scale * (pre_grad[pl.ds(at, rows), :] - sm - normed * gm)
        cg[pl.ds(at, rows), :] = jnp.where(ok, full, 0.0).astype(BF16).astype(F32)
        return 0

    lax.fori_loop(0, total // rows, grad, 0)
    part = rows_per_step(frames)
    part = part if part % 16 == 0 else frames

    def step(i, _):
        at = pl.multiple_of(i * part, 16)
        acc = [jnp.zeros((part, LANES), F32)]

        def add(k, window):
            acc[0] = acc[0] + taps[TAPS - 1 - k : TAPS - k, :] * window

        shifted_taps(lambda s, m: cg[pl.ds(at + s, m), :], part, add)
        ok = first + at + rows_iota(part) < length
        gg = jnp.where(ok, acc[0], 0.0)
        sig = sigmoid(gate[pl.ds(at, part), :].astype(F32))
        v = val[pl.ds(at, part), :].astype(F32)
        through = gg * sig
        out_val[pl.ds(at, part), :] = through.astype(BF16)
        out_gate[pl.ds(at, part), :] = (through * v * (1.0 - sig)).astype(BF16)
        return 0

    lax.fori_loop(0, frames // part, step, 0)


def columns(rows, at=0):
    return pl.BlockSpec((rows, LANES), lambda j: (0, j + at))


def everything(shape):
    return pl.BlockSpec(shape, lambda j: (0,) * len(shape))


SCALARS = pl.BlockSpec(memory_space=pltpu.SMEM)


def call(kernel, name, blocks, ins, outs, out_shapes, scratch=(), flops=10**9, nbytes=4 * 10**6):
    return pl.pallas_call(
        kernel,
        grid=(blocks,),
        in_specs=ins,
        out_specs=outs,
        out_shape=out_shapes,
        scratch_shapes=list(scratch),
        name=name,
        cost_estimate=pl.CostEstimate(flops=flops, bytes_accessed=nbytes, transcendentals=0),
        compiler_params=pltpu.CompilerParams(dimension_semantics=("arbitrary",)),
    )


def to_everyone(array, axis):
    size = lax.axis_size(axis)
    return lax.all_to_all(
        jnp.broadcast_to(array[None], (size, *array.shape)), axis, 0, 0, tiled=True
    )


def split_high_low(x):
    high = lax.reduce_precision(x, 8, 7)
    return high.astype(BF16), (x - high).astype(BF16)


def on_device(glu_input, out_grad, lengths, depth_weight, bn_gain, bn_shift, proj_weight):
    _, frames, doubled = glu_input.shape
    channels = doubled // 2
    width = out_grad.shape[2]
    blocks = channels // LANES
    seq_count, dp_count = lax.axis_size(SEQ), lax.axis_size("dp")
    tiles = lax.axis_size(XY)
    own = channels // seq_count
    wide_own = width // dp_count
    scale = float(dp_count * frames * seq_count) ** (-0.5)
    core = lax.axis_index("seq_2")
    first = lax.axis_index(SEQ) * frames
    length = lax.dynamic_index_in_dim(lengths, lax.axis_index("dp"), 0, keepdims=False)
    meta = jnp.stack([first.astype(jnp.int32), length])
    count = jnp.broadcast_to(jnp.sum(lengths).astype(F32), (8, LANES))
    x, grad = glu_input[0], out_grad[0]
    taps = jnp.pad(depth_weight.T, ((0, 1), (0, 0)))
    gain, shift = bn_gain.reshape(1, channels), bn_shift.reshape(1, channels)
    ext, conv_rows = frames + 2 * WIDE, frames + 2 * EDGE

    forward = [(i, i + 1) for i in range(seq_count - 1)]
    backward = [(j, i) for i, j in forward]
    low = lax.ppermute(jnp.concatenate([x[-WIDE:], grad[-EDGE:]], axis=0), SEQ, forward)
    high = lax.ppermute(jnp.concatenate([x[:WIDE], grad[:EDGE]], axis=0), SEQ, backward)

    weight = to_everyone(proj_weight, SEQ).reshape(channels, wide_own)
    weight = to_everyone(weight, "dp")

    glu, conv, stats = call(
        glu_kernel,
        "glu_conv",
        blocks,
        [SCALARS, columns(frames), columns(frames, blocks)]
        + [columns(WIDE + EDGE), columns(WIDE + EDGE, blocks)] * 2
        + [columns(TAPS + 1)],
        [columns(ext), columns(conv_rows), columns(2)],
        [
            jax.ShapeDtypeStruct((ext, channels), F32),
            jax.ShapeDtypeStruct((conv_rows, channels), F32),
            jax.ShapeDtypeStruct((2, channels), F32),
        ],
    )(meta, x, x, low, low, high, high, taps)

    stats = to_everyone(stats.reshape(2 * blocks, LANES), XY).sum(axis=0)
    stats = to_everyone(stats, CORE_DP)
    all_stats = everything(stats.shape)

    early = call(
        early_kernel,
        "early_terms",
        blocks,
        [SCALARS, columns(ext), columns(conv_rows)],
        pl.BlockSpec((2, TAPS + 1, LANES), lambda j: (0, 0, j)),
        jax.ShapeDtypeStruct((2, TAPS + 1, channels), F32),
        [pltpu.VMEM((8 * (TAPS + 1), LANES), F32)],
    )(meta, glu, conv)

    act_grad = call(
        act_grad_kernel,
        "act_grad",
        channels // 256,
        [
            everything((frames, width)),
            everything((WIDE + EDGE, width)),
            everything((WIDE + EDGE, width)),
            pl.BlockSpec((dp_count, 256, wide_own), lambda j: (0, j, 0)),
        ],
        pl.BlockSpec((conv_rows, 256), lambda j: (0, j)),
        jax.ShapeDtypeStruct((conv_rows, channels), F32),
    )(grad, low, high, weight)

    act, pre_grad, sums = call(
        pre_kernel,
        "pre_grad",
        blocks,
        [SCALARS, all_stats, everything((8, LANES)), columns(1), columns(1)]
        + [columns(conv_rows)] * 2,
        [columns(frames), columns(conv_rows), columns(2)],
        [
            jax.ShapeDtypeStruct((frames, channels), BF16),
            jax.ShapeDtypeStruct((conv_rows, channels), F32),
            jax.ShapeDtypeStruct((2, channels), F32),
        ],
        [pltpu.VMEM((2 * blocks, LANES), F32)],
    )(meta, stats, count, gain, shift, conv, act_grad)

    terms = jnp.einsum("tc,td->cd", act, grad, preferred_element_type=F32)
    terms = terms.reshape(tiles, 2, own, width)
    theirs = lax.dynamic_index_in_dim(terms, 1 - core, 1, keepdims=False).astype(BF16)
    theirs = lax.ppermute(theirs, "seq_2", [(0, 1), (1, 0)])
    mine = lax.dynamic_index_in_dim(terms, core, 1, keepdims=False)

    late = call(
        depth_kernel,
        "depth_terms",
        blocks,
        [SCALARS, columns(ext), columns(conv_rows)],
        columns(TAPS + 1),
        jax.ShapeDtypeStruct((TAPS + 1, channels), F32),
        [pltpu.VMEM((8 * (TAPS + 1), LANES), F32)],
    )(meta, glu, pre_grad)

    depth = jnp.concatenate([early, late[None]], axis=0).reshape(3, TAPS + 1, tiles, 2 * own)
    depth = depth.transpose(2, 0, 1, 3).reshape(tiles, -1)
    depth_size = depth.shape[1]
    small = jnp.concatenate([depth, jnp.broadcast_to(sums.reshape(1, -1), (tiles, 2 * channels))], 1)
    small_size = small.shape[1]
    both = jnp.concatenate(split_high_low(small), axis=1)
    room = -(-both.shape[1] // (own * LANES)) * LANES
    both = jnp.pad(both, ((0, 0), (0, own * room - both.shape[1]))).reshape(tiles, own, room)
    message = jnp.concatenate([(mine + theirs.astype(F32)).astype(BF16), both], axis=2)
    message = lax.all_to_all(message, XY, 0, 0, tiled=True).astype(F32).sum(axis=0)
    proj = message[:, :width]
    both = message[:, width:].reshape(-1)
    small = both[:small_size] + both[small_size : 2 * small_size]

    here = (jnp.arange(2) == core)[:, None, None, None]
    proj = proj.reshape(1, own, dp_count, wide_own).transpose(0, 2, 1, 3)
    proj = jnp.where(here, proj, 0.0).reshape(2 * dp_count, -1)
    depth = small[:depth_size].reshape(3 * (TAPS + 1), 2, own).transpose(1, 0, 2).reshape(2, 1, -1)
    depth = jnp.broadcast_to(depth, (2, dp_count, depth.shape[2])).reshape(2 * dp_count, -1)
    sums = jnp.broadcast_to(small[depth_size:][None], (2 * dp_count, 2 * channels))
    message = jnp.concatenate([proj, depth, sums], axis=1)
    size = message.shape[1]
    room = -(-size // 1024) * 1024
    message = jnp.pad(message, ((0, 0), (0, room - size))).reshape(2 * dp_count, room // LANES, LANES)
    message = lax.all_to_all(message, CORE_DP, 0, 0, tiled=True).sum(axis=0).reshape(-1)
    at = own * wide_own
    proj_grad = message[:at].reshape(own, wide_own) * scale
    depth = message[at : at + 3 * (TAPS + 1) * own].reshape(3, TAPS + 1, own)
    at += 3 * (TAPS + 1) * own
    sums = message[at : at + 2 * channels].reshape(2, channels)

    out_val, out_gate = call(
        last_kernel,
        "input_grad",
        blocks,
        [SCALARS, all_stats, everything((8, LANES)), columns(1), columns(2), columns(TAPS + 1)]
        + [columns(conv_rows)] * 2
        + [columns(frames), columns(frames, blocks)],
        [columns(frames)] * 2,
        [jax.ShapeDtypeStruct((frames, channels), BF16)] * 2,
        [pltpu.VMEM((conv_rows, LANES), F32), pltpu.VMEM((2 * blocks, LANES), F32)],
    )(meta, stats, count, gain, sums, taps, conv, pre_grad, x, x)
    input_grad = jnp.concatenate([out_val, out_gate], axis=1)[None]

    begin = lax.axis_index(SEQ) * own
    n = count[0, 0]
    total = stats.sum(axis=0).reshape(2, channels)
    total = lax.dynamic_slice_in_dim(total, begin, own, 1)
    mean = total[0] / n
    inv = lax.rsqrt(total[1] / n - mean * mean + EPSILON)
    sums = lax.dynamic_slice_in_dim(sums, begin, own, 1)
    own_gain = lax.dynamic_slice_in_dim(bn_gain, begin, own)
    flat, with_conv, with_grad = depth[0], depth[1], depth[2]
    depth_grad = with_grad - sums[1] / n * flat - sums[0] / n * inv * (with_conv - mean * flat)
    depth_grad = (depth_grad * (scale * inv * own_gain)).T[:, :TAPS]
    return (input_grad, proj_grad, depth_grad, sums[0] * scale, sums[1] * scale)


def solution(mesh):
    seq, dp = mesh.shape["seq"], mesh.shape["dp"]
    x = 4 if seq >= 64 else 2
    finer = Mesh(
        mesh.devices.reshape(x, seq // (2 * x), 2, dp), ("seq_0", "seq_1", "seq_2", "dp")
    )
    return jax.shard_map(
        on_device,
        mesh=finer,
        in_specs=(P("dp", SEQ, None), P("dp", SEQ, None), P(), P(), P(), P(), P(SEQ, "dp")),
        out_specs=(P("dp", SEQ, None), P(SEQ, "dp"), P(SEQ, None), P(SEQ), P(SEQ)),
        check_vma=False,
    )
```

time: 253 us -> 191 us (0.75)
  blocking collectives: 87.1 us -> 18.4 us
  Pallas kernels: 0 us -> 37.3 us
  other arithmetic: 36.5 us -> 9.51 us
  starting transfers between devices: 61.6 us -> 48.8 us
  waiting for transfers between devices: 49.2 us -> 56.8 us
  local copies, waits for them, and re-layouts: 10.1 us -> 16.3 us
  matrix products: 5.66 us -> 0.98 us
    psum x8 -> x0, blocking collectives: 87.1 us -> none  [by_axis(): array = lax.psum(array, axis)]
    pallas_call x0 -> x6, Pallas kernels: none -> 37.3 us  [the longest x1 8.36 us: on_device(): call(glu_kernel, 'glu_conv', blocks, [SCALARS, columns(frames), columns(f...]
    reduce_sum x7 -> x5, other arithmetic: 20.4 us -> 0.84 us  [the longest x1 0.63 us: on_device(): count = jnp.broadcast_to(jnp.sum(lengths).astype(F32), (8, LANES))]
    all_to_all x0 -> x1, blocking collectives: none -> 18.4 us  [to_everyone(): lax.all_to_all(jnp.broadcast_to(array[None], (size, *array.shape)), axis,...]
    ppermute x4 -> x3, starting transfers between devices: 17.6 us -> 9.03 us  [the longest x1 4.58 us: on_device(): lax.ppermute(jnp.concatenate([x[-WIDE:], grad[-EDGE:]], axis=0), SEQ, for...]
    all_to_all x5, waiting for transfers between devices: 47.5 us -> 55.3 us  [the longest x3 26.2 us: to_everyone(): lax.all_to_all(jnp.broadcast_to(array[None], (size, *array.shape)), axis,...]
    add x3 -> x1, other arithmetic: 6.16 us -> 0.01 us  [on_device(): small = both[:small_size] + both[small_size:2 * small_size]]
    dot_general x2 -> x1, matrix products: 5.66 us -> 0.98 us  [on_device(): terms = jnp.einsum('tc,td->cd', act, grad, preferred_element_type=F32)]
  transfers between devices with their start and end apart: 9 -> 8, of which waited for: 4 -> 4; matrix products, arithmetic and copies ran while one was open for 13% -> 4% of each run, Pallas kernels for 0% -> 10%
where the time goes in v1:
time: 191 us; the launch traced here: 190 us
  waiting for transfers between devices  56.8 us (30%)
  starting transfers between devices  48.8 us (26%)
  Pallas kernels  37.3 us (20%)
  blocking collectives  18.4 us (10%)
  local copies, waits for them, and re-layouts  16.3 us (9%)
  other arithmetic  9.51 us (5%)
    all_to_all x3, waiting for transfers between devices, to_everyone(): lax.all_to_all(jnp.broadcast_to(array[None], (size, *array.shape)), axis,...  26.2 us
    all_to_all x3, starting transfers between devices, to_everyone(): lax.all_to_all(jnp.broadcast_to(array[None], (size, *array.shape)), axis,...  24.8 us
    all_to_all x1, waiting for transfers between devices, on_device(): lax.all_to_all(message, XY, 0, 0, tiled=True).astype(F32).sum(axis=0)  20.8 us
    all_to_all x1, blocking collectives, to_everyone(): lax.all_to_all(jnp.broadcast_to(array[None], (size, *array.shape)), axis,...  18.4 us
    all_to_all x1, starting transfers between devices, on_device(): lax.all_to_all(message, CORE_DP, 0, 0, tiled=True).sum(axis=0).reshape(-1)  10.6 us
    pallas_call x1, Pallas kernels, on_device(): call(glu_kernel, 'glu_conv', blocks, [SCALARS, columns(frames), columns(f...  8.36 us
    all_to_all x1, waiting for transfers between devices, on_device(): lax.all_to_all(message, CORE_DP, 0, 0, tiled=True).sum(axis=0).reshape(-1)  8.23 us
    pallas_call x1, Pallas kernels, on_device(): call(last_kernel, 'input_grad', blocks, [SCALARS, all_stats, everything((...  7.86 us
  transfers between devices with their start and end apart: 8, of which 4 were waited for; matrix products, arithmetic and copies ran while one was open for 4% of the time, Pallas kernels for 10%

profile of v1, /device:TPU:1, one launch (start us, length us, event | category | flops | bytes accessed | tf_op | source)
XLA Modules:
  0.0 189.7 jit_solution(3105064562341689374)
XLA Ops:
  0.6 0.8 slice_bitcast_fusion.4
  1.4 0.9 slice_bitcast_fusion.1
  2.3 4.6 %collective-permute-start = (bf16[48,1024]{1,0:T(8,128)(2,1)S(1)}, bf16[48,1024]{1,0:T(8,128)(2,1)S(1)}, u32[]{:S(2)}, u32[]{:S(2)}) collective-permute-start(bf16[48,1024]{1,0:T(8,128)(2,1)S(1)} %pad_maximum_fusion.1), channel_id=1, source_target_pairs={{0,8},{8,16},{16,24},{24,32},{32,40},{40,48},{48,56},{56,64},{64,7... | collective-permute-start | bytes 294920 | tf_op jit(solution)/shard_map/ppermute | solution.py:299
  6.9 1.4 broadcast_in_dim.93
  8.3 9.3 %all-to-all-start.2 = ((bf16[64,8,128]{2,1,0:T(8,128)(2,1)}), bf16[64,8,128]{2,1,0:T(8,128)(2,1)S(1)}, u32[]{:S(2)}, u32[]{:S(2)}) async-start(bf16[64,8,128]{2,1,0:T(8,128)(2,1)} %broadcast_in_dim.93), calls=%async_computation.2 | async-start | bytes 262144 | tf_op jit(solution)/shard_map/all_to_all | solution.py:267
  17.6 2.4 %collective-permute-start.1 = (bf16[48,1024]{1,0:T(8,128)(2,1)S(1)}, bf16[48,1024]{1,0:T(8,128)(2,1)S(1)}, u32[]{:S(2)}, u32[]{:S(2)}) collective-permute-start(bf16[48,1024]{1,0:T(8,128)(2,1)S(1)} %pad_maximum_fusion.2), channel_id=1, source_target_pairs={{8,0},{16,8},{24,16},{32,24},{40,32},{48,40},{56,48},{64,56},{72,6... | collective-permute-start | bytes 294920 | tf_op jit(solution)/shard_map/ppermute | solution.py:300
  20.0 1.2 dynamic_slice.20
  21.2 1.5 pad.8.taps
  22.7 1.3 pad_add_fusion.meta
  24.0 0.0 collective-permute-done.1.high_val.high_gate.high
  24.1 0.6 copy-done.5
  24.7 0.0 copy-done.6
  24.7 8.4 %glu_conv.1 = (f32[832,512]{1,0:T(8,128)}, f32[800,512]{1,0:T(8,128)}, f32[2,512]{1,0:T(2,128)}) custom-call(s32[2]{0:T(128)} %pad_add_fusion.meta, bf16[768,1024]{1,0:T(8,128)(2,1)} %bitcast.68, bf16[768,1024]{1,0:T(8,128)(2,1)} %bitcast.69, bf16[48,1024]{1,0:T(8,128)(2,1)} %copy-done.5, bf16[48,1024]{1,0:T(8,128)(2,1)} %copy-done.5, ...), custom_call_target="tpu_custom_call" | custom-call | flops 1000000000 | bytes 4000000 | tf_op jit(solution)/shard_map/glu_conv/pallas_call | solution.py:305
  33.1 0.7 broadcast_in_dim.86
  33.8 18.4 %all_to_all.30 = f32[32,8,128]{2,1,0:T(8,128)S(1)} all-to-all(f32[32,8,128]{2,1,0:T(8,128)S(1)} %broadcast_in_dim.87), channel_id=1, replica_groups=mesh['seq_0'=4,'seq_1'=8,'seq_2'=2,'dp'=8] {'seq_0','seq_1'}, dimensions={0} | all-to-all | bytes 262144 | tf_op jit(solution)/shard_map/all_to_all | solution.py:267
  52.2 1.1 broadcast_in_dim.95
  53.3 10.0 %all-to-all-start.3 = ((bf16[8,512,128]{2,1,0:T(8,128)(2,1)}), bf16[8,512,128]{2,1,0:T(8,128)(2,1)S(1)}, u32[]{:S(2)}, u32[]{:S(2)}) async-start(bf16[8,512,128]{2,1,0:T(8,128)(2,1)} %broadcast_in_dim.95), calls=%async_computation.3 | async-start | bytes 2097152 | tf_op jit(solution)/shard_map/all_to_all | solution.py:267
  63.3 0.6 reduce_sum.46
  64.6 26.2 %all-to-all-done.3.weight = bf16[8,512,128]{2,1,0:T(8,128)(2,1)S(1)} async-done(((bf16[8,512,128]{2,1,0:T(8,128)(2,1)}), bf16[8,512,128]{2,1,0:T(8,128)(2,1)S(1)}, u32[]{:S(2)}, u32[]{:S(2)}) %all-to-all-start.3) | async-done | bytes 1048608 | tf_op jit(solution)/shard_map/all_to_all | solution.py:267
  90.9 0.7 broadcast_in_dim.88
  91.5 5.4 %all-to-all-start.1 = ((f32[16,8,128]{2,1,0:T(8,128)}), f32[16,8,128]{2,1,0:T(8,128)S(1)}, u32[]{:S(2)}, u32[]{:S(2)}) async-start(f32[16,8,128]{2,1,0:T(8,128)} %broadcast_in_dim.88), calls=%async_computation.1 | async-start | bytes 131072 | tf_op jit(solution)/shard_map/all_to_all | solution.py:267
  97.0 6.2 %early_terms.1 = f32[2,32,512]{2,1,0:T(8,128)} custom-call(s32[2]{0:T(128)} %pad_add_fusion.meta, f32[832,512]{1,0:T(8,128)} %get-tuple-element.16.glu, f32[800,512]{1,0:T(8,128)} %get-tuple-element.14.conv), custom_call_target="tpu_custom_call" | custom-call | flops 1000000000 | bytes 4000000 | tf_op jit(solution)/shard_map/early_terms/pallas_call | solution.py:324
  103.2 1.1 copy.30
  104.3 4.1 %act_grad.1 = f32[800,512]{1,0:T(8,128)} custom-call(bf16[768,1024]{1,0:T(8,128)(2,1)} %bitcast.74, bf16[48,1024]{1,0:T(8,128)(2,1)} %copy-done.5, bf16[48,1024]{1,0:T(8,128)(2,1)} %copy-done.6, bf16[8,512,128]{2,1,0:T(8,128)(2,1)} %copy-done), custom_call_target="tpu_custom_call" | custom-call | flops 1000000000 | bytes 4000000 | tf_op jit(solution)/shard_map/act_grad/pallas_call | solution.py:334
  108.4 0.6 broadcast_in_dim.89.count
  109.0 0.0 copy-done.3
  109.0 4.9 %pre_grad.1 = (bf16[768,512]{1,0:T(8,128)(2,1)}, f32[800,512]{1,0:T(8,128)}, f32[2,512]{1,0:T(2,128)}) custom-call(s32[2]{0:T(128)} %pad_add_fusion.meta, f32[16,8,128]{2,1,0:T(8,128)} %copy-done.3, f32[8,128]{1,0:T(8,128)} %broadcast_in_dim.89.count, f32[1,512]{1,0:T(1,128)} %bitcast.83, f32[1,512]{1,0:T(1,128)} %bitcast.86, ...), custom_call_target="tpu_custom_call" | custom-call | flops 1000000000 | bytes 4000000 | tf_op jit(solution)/shard_map/pre_grad/pallas_call | solution.py:348
  113.9 5.8 %depth_terms.1 = f32[32,512]{1,0:T(8,128)} custom-call(s32[2]{0:T(128)} %pad_add_fusion.meta, f32[832,512]{1,0:T(8,128)} %get-tuple-element.16.glu, f32[800,512]{1,0:T(8,128)} %get-tuple-element.17.pre_grad), custom_call_target="tpu_custom_call" | custom-call | flops 1000000000 | bytes 4000000 | tf_op jit(solution)/shard_map/depth_terms/pallas_call | solution.py:369
  119.8 1.0 copy.31
  120.8 0.0 copy-start.8
  120.8 0.1 maximum_bitcast_fusion.1
  120.8 0.0 copy-start.1
  120.9 0.5 copy.32
  121.4 0.2 copy.33
  121.6 1.4 copy.29
  123.1 1.0 fusion
  124.1 0.1 fusion.3
  124.1 2.1 %collective-permute-start.2 = (bf16[32,8,1024]{2,1,0:T(8,128)(2,1)S(1)}, bf16[32,8,1024]{2,1,0:T(8,128)(2,1)S(1)}, u32[]{:S(2)}, u32[]{:S(2)}) collective-permute-start(bf16[32,8,1024]{2,1,0:T(8,128)(2,1)S(1)} %fusion.3), channel_id=1, source_target_pairs={{0,8},{8,0},{1,9},{9,1},{2,10},{10,2},{3,11},{11,3},{4,12},{12,4},... | collective-permute-start | bytes 1572872 | tf_op jit(solution)/shard_map/ppermute | solution.py:366
  126.3 0.1 concatenate.38
  126.4 0.1 reduce-precision_convert_fusion
  126.5 1.4 collective-permute-done.2
  127.9 1.4 fusion.2
  129.3 1.1 maximum_maximum_fusion
  130.4 4.4 %all-to-all-start.4 = ((bf16[32,8,1664]{2,1,0:T(8,128)(2,1)}), bf16[32,8,1664]{2,1,0:T(8,128)(2,1)S(1)}, u32[]{:S(2)}, u32[]{:S(2)}) async-start(bf16[32,8,1664]{2,1,0:T(8,128)(2,1)} %maximum_maximum_fusion), calls=%async_computation.4 | async-start | bytes 1703936 | tf_op jit(solution)/shard_map/all_to_all | solution.py:388
  134.8 0.1 broadcast_in_dim.90
  134.9 0.1 broadcast_in_dim.91
  135.0 20.8 %all-to-all-done.4 = bf16[32,8,1664]{2,1,0:T(8,128)(2,1)S(1)} async-done(((bf16[32,8,1664]{2,1,0:T(8,128)(2,1)}), bf16[32,8,1664]{2,1,0:T(8,128)(2,1)S(1)}, u32[]{:S(2)}, u32[]{:S(2)}) %all-to-all-start.4) | async-done | bytes 852000 | tf_op jit(solution)/shard_map/all_to_all | solution.py:388
  155.8 0.1 convert_reduce_fusion
  156.0 0.3 add.56
  156.3 0.1 broadcast_in_dim.102
  156.5 0.1 bitcast_select_fusion
  156.6 0.7 copy.39
  157.3 10.6 %all-to-all-start.5 = ((f32[16,24,128]{2,1,0:T(8,128)}), f32[16,24,128]{2,1,0:T(8,128)S(1)}, u32[]{:S(2)}, u32[]{:S(2)}) async-start(f32[16,24,128]{2,1,0:T(8,128)} %bitcast.42), calls=%async_computation.5 | async-start | bytes 393216 | tf_op jit(solution)/shard_map/all_to_all | solution.py:403
  168.0 8.2 %all-to-all-done.5 = f32[16,24,128]{2,1,0:T(8,128)S(1)} async-done(((f32[16,24,128]{2,1,0:T(8,128)}), f32[16,24,128]{2,1,0:T(8,128)S(1)}, u32[]{:S(2)}, u32[]{:S(2)}) %all-to-all-start.5) | async-done | bytes 196640 | tf_op jit(solution)/shard_map/all_to_all | solution.py:403
  176.2 0.6 slice_multiply_fusion
  176.8 0.1 squeeze.34
  176.9 0.1 squeeze.33
  177.0 0.1 squeeze.32
  177.1 0.1 constant_dynamic-slice_fusion
  177.2 0.5 multiply_bitcast_fusion.1
  177.7 0.8 bitcast_multiply_fusion
  178.5 0.7 copy.36
  179.1 7.9 %input_grad.1 = (bf16[768,512]{1,0:T(8,128)(2,1)}, bf16[768,512]{1,0:T(8,128)(2,1)}) custom-call(s32[2]{0:T(128)} %pad_add_fusion.meta, f32[16,8,128]{2,1,0:T(8,128)} %copy-done.3, f32[8,128]{1,0:T(8,128)} %broadcast_in_dim.89.count, f32[1,512]{1,0:T(1,128)} %bitcast.84, f32[2,512]{1,0:T(2,128)} %copy-done.7, f32[32,512]{1,0:T(8,128)} %pad.8.taps, ...), custom_call_target="tpu_custom_call" | custom-call | flops 1000000000 | bytes 4000000 | tf_op jit(solution)/shard_map/input_grad/pallas_call | solution.py:410
  187.0 2.7 %maximum_bitcast_fusion = bf16[1,768,1024]{2,1,0:T(8,128)(2,1)} fusion(bf16[768,512]{1,0:T(8,128)(2,1)} %get-tuple-element.20, bf16[768,512]{1,0:T(8,128)(2,1)} %get-tuple-element.19), kind=kLoop, calls=%fused_computation.1 | loop fusion | flops 3145728 | bytes 3145728 | tf_op jit(solution)/shard_map/broadcast_in_dim | solution.py:421
  (43 shorter events, 0.3 us)
Async XLA Ops:
  2.3 21.7 %collective-permute-start = (bf16[48,1024]{1,0:T(8,128)(2,1)S(1)}, bf16[48,1024]{1,0:T(8,128)(2,1)S(1)}, u32[]{:S(2)}, u32[]{:S(2)}) collective-permute-start(bf16[48,1024]{1,0:T(8,128)(2,1)S(1)} %pad_maximum_fusion.1), channel_id=1, source_target_pairs={{0,8},{8,16},{16,24},{24,32},{32,40},{40,48},{48,56},{56,64},{64,7... | collective-permute-start | bytes 294920 | tf_op jit(solution)/shard_map/ppermute | solution.py:299
  8.3 25.5 %all-to-all-start.2 = ((bf16[64,8,128]{2,1,0:T(8,128)(2,1)}), bf16[64,8,128]{2,1,0:T(8,128)(2,1)S(1)}, u32[]{:S(2)}, u32[]{:S(2)}) async-start(bf16[64,8,128]{2,1,0:T(8,128)(2,1)} %broadcast_in_dim.93), calls=%async_computation.2 | async-start | bytes 262144 | tf_op jit(solution)/shard_map/all_to_all | solution.py:267
  17.6 6.4 %collective-permute-start.1 = (bf16[48,1024]{1,0:T(8,128)(2,1)S(1)}, bf16[48,1024]{1,0:T(8,128)(2,1)S(1)}, u32[]{:S(2)}, u32[]{:S(2)}) collective-permute-start(bf16[48,1024]{1,0:T(8,128)(2,1)S(1)} %pad_maximum_fusion.2), channel_id=1, source_target_pairs={{8,0},{16,8},{24,16},{32,24},{40,32},{48,40},{56,48},{64,56},{72,6... | collective-permute-start | bytes 294920 | tf_op jit(solution)/shard_map/ppermute | solution.py:300
  24.0 0.7 copy-start.5
  24.1 0.6 copy-start.6
  52.2 11.1 %copy-start.9 = (s32[8]{0:T(128)S(1)}, s32[8]{0:T(128)}, u32[]{:S(2)}) copy-start(s32[8]{0:T(128)} %param.9) | copy-start | bytes 100
  53.3 37.6 %all-to-all-start.3 = ((bf16[8,512,128]{2,1,0:T(8,128)(2,1)}), bf16[8,512,128]{2,1,0:T(8,128)(2,1)S(1)}, u32[]{:S(2)}, u32[]{:S(2)}) async-start(bf16[8,512,128]{2,1,0:T(8,128)(2,1)} %broadcast_in_dim.95), calls=%async_computation.3 | async-start | bytes 2097152 | tf_op jit(solution)/shard_map/all_to_all | solution.py:267
  90.9 12.4 %copy-start = (bf16[8,512,128]{2,1,0:T(8,128)(2,1)}, bf16[8,512,128]{2,1,0:T(8,128)(2,1)S(1)}, u32[]{:S(2)}) copy-start(bf16[8,512,128]{2,1,0:T(8,128)(2,1)S(1)} %all-to-all-done.3.weight) | copy-start | bytes 3145732
  91.5 16.9 %all-to-all-start.1 = ((f32[16,8,128]{2,1,0:T(8,128)}), f32[16,8,128]{2,1,0:T(8,128)S(1)}, u32[]{:S(2)}, u32[]{:S(2)}) async-start(f32[16,8,128]{2,1,0:T(8,128)} %broadcast_in_dim.88), calls=%async_computation.1 | async-start | bytes 131072 | tf_op jit(solution)/shard_map/all_to_all | solution.py:267
  108.4 0.6 copy-start.3
  120.8 0.9 copy-start.8
  120.8 2.2 %copy-start.1 = (bf16[1,768,1024]{2,1,0:T(8,128)(2,1)S(1)}, bf16[1,768,1024]{2,1,0:T(8,128)(2,1)}, u32[]{:S(2)}) copy-start(bf16[1,768,1024]{2,1,0:T(8,128)(2,1)} %param.8) | copy-start | bytes 4718596
  124.0 2.2 %copy-start.2 = (f32[32,2,8,1024]{3,2,1,0:T(8,128)}, f32[32,2,8,1024]{3,2,1,0:T(8,128)S(1)}, u32[]{:S(2)}) copy-start(f32[32,2,8,1024]{3,2,1,0:T(8,128)S(1)} %fusion) | copy-start | bytes 6291460
  124.1 3.8 %collective-permute-start.2 = (bf16[32,8,1024]{2,1,0:T(8,128)(2,1)S(1)}, bf16[32,8,1024]{2,1,0:T(8,128)(2,1)S(1)}, u32[]{:S(2)}, u32[]{:S(2)}) collective-permute-start(bf16[32,8,1024]{2,1,0:T(8,128)(2,1)S(1)} %fusion.3), channel_id=1, source_target_pairs={{0,8},{8,0},{1,9},{9,1},{2,10},{10,2},{3,11},{11,3},{4,12},{12,4},... | collective-permute-start | bytes 1572872 | tf_op jit(solution)/shard_map/ppermute | solution.py:366
  130.4 25.4 %all-to-all-start.4 = ((bf16[32,8,1664]{2,1,0:T(8,128)(2,1)}), bf16[32,8,1664]{2,1,0:T(8,128)(2,1)S(1)}, u32[]{:S(2)}, u32[]{:S(2)}) async-start(bf16[32,8,1664]{2,1,0:T(8,128)(2,1)} %maximum_maximum_fusion), calls=%async_computation.4 | async-start | bytes 1703936 | tf_op jit(solution)/shard_map/all_to_all | solution.py:388
  135.0 32.9 %copy-start.4 = (f32[16,8,128]{2,1,0:T(8,128)S(1)}, f32[16,8,128]{2,1,0:T(8,128)}, u32[]{:S(2)}) copy-start(f32[16,8,128]{2,1,0:T(8,128)} %copy-done.3) | copy-start | bytes 196612
  157.3 18.9 %all-to-all-start.5 = ((f32[16,24,128]{2,1,0:T(8,128)}), f32[16,24,128]{2,1,0:T(8,128)S(1)}, u32[]{:S(2)}, u32[]{:S(2)}) async-start(f32[16,24,128]{2,1,0:T(8,128)} %bitcast.42), calls=%async_computation.5 | async-start | bytes 393216 | tf_op jit(solution)/shard_map/all_to_all | solution.py:403
  176.8 2.3 %copy-start.7 = (f32[2,512]{1,0:T(2,128)}, f32[2,512]{1,0:T(2,128)S(1)}, u32[]{:S(2)}) copy-start(f32[2,512]{1,0:T(2,128)S(1)} %reshape.111.sums) | copy-start | bytes 12292
